TPU v7x, 32 devices: a whole 2x2x4 slice. The times are simulated.
32 devices in a mesh: dp: 2 (over x), tensor: 4 (over y, core), grid: 4 (over z).
Axes of the slice: x: 2, y: 2, z: 4, core: 2. Of those that a mesh axis runs over, the one named last changes fastest.
Arguments:
- tokens: bfloat16 [1536, 8192], P('dp', 'grid'), may hold values from -6 to 6
- cotangents: bfloat16 [2, 1536, 1024], P(None, 'dp', 'tensor'), may hold values from -0.03125 to 0.03125
- left_stat: float32 [2, 8192, 8192], P(None, ('dp', 'tensor'), 'grid'), may hold values from -6 to 6
- right_stat: float32 [2, 1024, 1024], P(None, ('dp', 'tensor'), 'grid'), may hold values from -6 to 6
- left_root: bfloat16 [2, 8192, 8192], P(None, ('dp', 'tensor'), 'grid'), may hold values from -0.3125 to 0.3125
- right_root: bfloat16 [2, 1024, 1024], P(None, 'grid'), as said below
- momentum: float32 [2, 8192, 1024], P(None, ('dp', 'tensor', 'grid')), may hold values from -6 to 6
Outputs:
- new_left: float32 [2, 8192, 8192], P(None, ('dp', 'tensor'), 'grid')
- new_right: float32 [2, 1024, 1024], P(None, ('dp', 'tensor'), 'grid')
- new_momentum: float32 [2, 8192, 1024], P(None, ('dp', 'tensor', 'grid'))
Inputs may be any that keep to these rules, and one draw needn't show every extreme that they name: `right_root`: each of the two factors is exactly symmetric.
All inputs are finite; a program needn't handle non-finite values.
Results may differ from a plain program's by a relative error of at most 0.0023.
Values may be sent and summed in bfloat16 or wider, within the bound.
No kernel may reach another device: no remote copies, remote signals or barrier semaphores. Data moves between devices by JAX's collectives and lax.ppermute only.
A program may use at most 128 MiB of HBM per device.

v0:
```python
import jax
import jax.numpy as jnp
from jax import lax
from jax.sharding import PartitionSpec as P

stat_decay = 0.9
momentum_decay = 0.9


def spread(shard, axis, root):
    mine = lax.axis_index(axis) == root
    return lax.psum(jnp.where(mine, shard, jnp.zeros_like(shard)), axis)


def shards(tokens, cotangents, left_stat, right_stat, left_root, right_root, momentum):
    partial_grad = jnp.einsum("tr,pto->pro", tokens, cotangents, preferred_element_type=jnp.float32)
    summed = lax.psum(partial_grad, "dp")
    grad_rows = lax.all_gather(summed.astype(jnp.bfloat16), "tensor", axis=2, tiled=True)
    block_rows = left_stat.shape[1]
    grid_rows = left_stat.shape[2]
    learner = lax.axis_index("dp") * lax.axis_size("tensor") + lax.axis_index("tensor")
    first_row = learner * block_rows
    source = first_row // grid_rows
    offset = first_row % grid_rows
    selected = lax.dynamic_slice_in_dim(grad_rows, offset, block_rows, 1)
    own_rows = spread(selected, "grid", source)
    gram_left = jnp.einsum("pak,pbk->pab", own_rows, grad_rows, preferred_element_type=jnp.float32)
    new_left = stat_decay * left_stat + (1.0 - stat_decay) * gram_left
    column_width = right_stat.shape[2]
    column_block = lax.dynamic_slice_in_dim(
        own_rows, lax.axis_index("grid") * column_width, column_width, 2
    )
    right_term = jnp.einsum(
        "pak,pac->pkc", own_rows, column_block, preferred_element_type=jnp.float32
    )
    gram_right = lax.psum_scatter(right_term, ("dp", "tensor"), scatter_dimension=1, tiled=True)
    new_right = stat_decay * right_stat + (1.0 - stat_decay) * gram_right
    applied = lax.psum_scatter(
        jnp.einsum("pab,pbk->apk", left_root, grad_rows, preferred_element_type=jnp.float32),
        "grid",
        scatter_dimension=0,
        tiled=True,
    )
    widened_rows = lax.all_gather(right_root, "grid", axis=1, tiled=True).astype(jnp.float32)
    update = jnp.einsum(
        "mpk,pkc->mpc",
        applied,
        widened_rows,
        precision=lax.Precision.HIGHEST,
        preferred_element_type=jnp.float32,
    )
    new_momentum = momentum_decay * momentum + jnp.transpose(update, (1, 0, 2))
    return (new_left, new_right, new_momentum)


def solution(mesh):
    return jax.shard_map(
        shards,
        mesh=mesh,
        in_specs=(
            P("dp", "grid"),
            P(None, "dp", "tensor"),
            P(None, ("dp", "tensor"), "grid"),
            P(None, ("dp", "tensor"), "grid"),
            P(None, ("dp", "tensor"), "grid"),
            P(None, "grid", None),
            P(None, ("dp", "tensor", "grid"), None),
        ),
        out_specs=(
            P(None, ("dp", "tensor"), "grid"),
            P(None, ("dp", "tensor"), "grid"),
            P(None, ("dp", "tensor", "grid"), None),
        ),
        check_vma=False,
    )
```

profile of v0, /device:TPU:0, one launch (start us, length us, event | category | flops | bytes accessed | tf_op | source)
XLA Modules:
  0.0 623.4 jit_solution(15898698768469071698)
XLA Ops:
  7.2 0.0 copy-start
  7.2 0.0 all-gather.3.cloned.1.call-start
  7.2 1.8 copy-done
  9.1 5.0 convolution_bitcast_fusion
  14.0 102.3 %all-reduce.4 = bf16[2,2048,256]{1,2,0:T(8,128)(2,1)} all-reduce(f32[2,2048,256]{1,2,0:T(8,128)} %convolution_bitcast_fusion), channel_id=1, replica_groups=mesh['dp'=2,'tensor'=4,'grid'=4] {'dp'}, use_global_device_ids=true, to_apply=%region_0.0 | all-reduce | flops 1048576 | bytes 6291456 | tf_op jit(solution)/shard_map/psum | solution.py:17
  116.3 0.0 all-gather.3.cloned.1.call-update
  116.3 0.0 all-reduce.3.cloned.1.call-start
  116.4 58.7 %all-gather.3.cloned.1.call-done = bf16[2,2048,1024]{1,2,0:T(8,128)(2,1)} async-done(((bf16[2,2048,256]{1,2,0:T(8,128)(2,1)}), bf16[2,2048,1024]{1,2,0:T(8,128)(2,1)}) %all-gather.3.cloned.1.call-update) | async-done | bytes 8388624 | tf_op jit(solution)/shard_map/all_gather | solution.py:18
  175.1 5.5 dynamic-slice_select_fusion
  180.5 0.0 all-reduce.3.cloned.1.call-update
  180.6 0.0 reduce-scatter.3.cloned.1.call-start
  180.6 155.1 %all-reduce.3.cloned.1.call-done = bf16[2,1024,1024]{1,2,0:T(8,128)(2,1)} async-done(((bf16[2,1024,1024]{1,2,0:T(8,128)(2,1)}), bf16[2,1024,1024]{1,2,0:T(8,128)(2,1)}) %all-reduce.3.cloned.1.call-update) | async-done | bytes 4194320 | tf_op jit(solution)/shard_map/psum | solution.py:12
  335.7 5.1 fusion.1
  340.8 0.0 reduce-scatter.3.cloned.1.call-update
  340.8 0.0 all-gather.5.cloned.1.call-start
  340.9 0.5 all-gather.5.cloned.1.call-update
  341.4 0.2 reduce-scatter.5.cloned.1.call-start
  341.6 15.9 %convolution_bitcast_fusion.1 = f32[1024,2,1024]{2,0,1:T(8,128)} fusion(bf16[2,2048,1024]{1,2,0:T(8,128)(2,1)} %all-gather.3.cloned.1.call-done, bf16[2,1024,2048]{2,1,0:T(8,128)(2,1)} %param.11), kind=kOutput, calls=%fused_computation.3 | convolution fusion | flops 8589934592 | bytes 25165824 | tf_op jit(solution)/shard_map/pab,pbk->apk/dot_general | solution.py:39
  357.5 0.0 reduce-scatter.5.cloned.1.call-update
  357.6 0.0 copy-start.2
  357.6 20.4 %multiply_add_fusion = f32[2,1024,2048]{2,1,0:T(8,128)} fusion(f32[2,1024,2048]{2,1,0:T(8,128)} %param.9, bf16[2,1024,1024]{1,2,0:T(8,128)(2,1)} %all-reduce.3.cloned.1.call-done, bf16[2,2048,1024]{1,2,0:T(8,128)(2,1)} %all-gather.3.cloned.1.call-done), kind=kOutput, calls=%fused_computation | convolution fusion | flops 8602517504 | bytes 46137344 | tf_op jit(solution)/shard_map/pak,pbk->pab/dot_general | solution.py:27
  378.0 3.0 reduce-scatter.3.cloned.1.call-done
  381.1 0.0 copy-done.2
  381.1 0.0 copy-start.1
  381.1 1.8 multiply_add_fusion.2
  382.9 80.3 %all-gather.5.cloned.1.call-done = bf16[2,1024,1024]{2,1,0:T(8,128)(2,1)} async-done(((bf16[2,256,1024]{2,1,0:T(8,128)(2,1)}), bf16[2,1024,1024]{2,1,0:T(8,128)(2,1)}) %all-gather.5.cloned.1.call-update) | async-done | bytes 4194320 | tf_op jit(solution)/shard_map/all_gather | solution.py:44
  463.2 145.3 %reduce-scatter.5.cloned.1.call-done = f32[256,2,1024]{2,0,1:T(8,128)} async-done(((f32[1024,2,1024]{2,0,1:T(8,128)}), f32[256,2,1024]{2,0,1:T(8,128)}) %reduce-scatter.5.cloned.1.call-update) | async-done | bytes 2097168 | tf_op jit(solution)/shard_map/reduce_scatter | solution.py:38
  608.6 8.3 %multiply_add_fusion.1 = f32[2,256,1024]{2,1,0:T(8,128)} fusion(f32[2,256,1024]{2,1,0:T(8,128)} %param.13, f32[256,2,1024]{2,0,1:T(8,128)} %reduce-scatter.5.cloned.1.call-done, bf16[2,1024,1024]{2,1,0:T(8,128)(2,1)} %all-gather.5.cloned.1.call-done), kind=kOutput, calls=%fused_computation.5 | convolution fusion | flops 6443499520 | bytes 10485760 | tf_op jit(solution)/shard_map/mpk,pkc->mpc/dot_general | solution.py:45
  616.9 0.0 copy-done.1
Async XLA Ops:
  7.2 1.9 copy-start
  7.2 167.9 %all-gather.3.cloned.1.call-start = ((), (), s32[]{:S(2)}) async-start(), calls=%async_computation.2 | async-start | bytes 10485760 | tf_op jit(solution)/shard_map/all_gather | solution.py:18
  116.3 219.4 %all-reduce.3.cloned.1.call-start = ((), (), s32[]{:S(2)}) async-start(), calls=%async_computation.3 | async-start | bytes 8388608 | tf_op jit(solution)/shard_map/psum | solution.py:12
  180.6 200.5 %reduce-scatter.3.cloned.1.call-start = ((), (), s32[]{:S(2)}) async-start(), calls=%async_computation.4 | async-start | bytes 2359296 | tf_op jit(solution)/shard_map/reduce_scatter | solution.py:36
  340.8 122.4 %all-gather.5.cloned.1.call-start = ((), (), s32[]{:S(2)}) async-start(), calls=%async_computation.6 | async-start | bytes 5242880 | tf_op jit(solution)/shard_map/all_gather | solution.py:44
  341.4 267.2 %reduce-scatter.5.cloned.1.call-start = ((), (), s32[]{:S(2)}) async-start(), calls=%async_computation.5 | async-start | bytes 10485760 | tf_op jit(solution)/shard_map/reduce_scatter | solution.py:38
  357.6 23.5 %copy-start.2 = (f32[2,128,256]{2,1,0:T(8,128)S(1)}, f32[2,128,256]{2,1,0:T(8,128)}, u32[]{:S(2)}) copy-start(f32[2,128,256]{2,1,0:T(8,128)} %param.10) | copy-start | bytes 786436
  381.1 235.8 %copy-start.1 = (bf16[768,2048]{1,0:T(8,128)(2,1)S(1)}, bf16[768,2048]{1,0:T(8,128)(2,1)}, u32[]{:S(2)}) copy-start(bf16[768,2048]{1,0:T(8,128)(2,1)} %param.7) | copy-start | bytes 9437188
Sparse Core Ops, SparseCore 0:
  116.4 58.5 all-gather.2
  180.7 154.9 all-reduce.2
  340.9 40.0 reduce-scatter.2
  382.5 80.7 all-gather.4
  465.4 143.0 reduce-scatter.4
where the time goes:
time: 624 us; the launch traced here: 623 us
  waiting for transfers between devices  443 us (71%)
  blocking collectives  102 us (16%)
  matrix products  54.7 us (9%)
  between operations  13.8 us (2%)
  other arithmetic  7.33 us (1%)
    psum x1, waiting for transfers between devices, spread(): return lax.psum(jnp.where(mine, shard, jnp.zeros_like(shard)), axis)  155 us
    reduce_scatter x1, waiting for transfers between devices, shards(): lax.psum_scatter(jnp.einsum('pab,pbk->apk', left_root, grad_rows, preferr...  145 us
    psum x1, blocking collectives, shards(): summed = lax.psum(partial_grad, 'dp')  102 us
    all_gather x1, waiting for transfers between devices, shards(): lax.all_gather(right_root, 'grid', axis=1, tiled=True).astype(jnp.float32)  80.3 us
    all_gather x1, waiting for transfers between devices, shards(): lax.all_gather(summed.astype(jnp.bfloat16), 'tensor', axis=2, tiled=True)  58.7 us
    dot_general x1, matrix products, shards(): jnp.einsum('pak,pbk->pab', own_rows, grad_rows, preferred_element_type=jn...  20.4 us
    dot_general x1, matrix products, shards(): jnp.einsum('pab,pbk->apk', left_root, grad_rows, preferred_element_type=j...  15.9 us
  transfers between devices with their start and end apart: 5, of which 5 were waited for; matrix products, arithmetic and copies ran while one was open for 6% of the time, Pallas kernels for 0%

commit v1 on v0

--- a/solution.py
+++ b/solution.py
@@ -14,7 +14,7 @@
 
 def shards(tokens, cotangents, left_stat, right_stat, left_root, right_root, momentum):
     partial_grad = jnp.einsum("tr,pto->pro", tokens, cotangents, preferred_element_type=jnp.float32)
-    summed = lax.psum(partial_grad, "dp")
+    summed = jnp.sum(lax.all_gather(partial_grad, "dp"), axis=0)
     grad_rows = lax.all_gather(summed.astype(jnp.bfloat16), "tensor", axis=2, tiled=True)
     block_rows = left_stat.shape[1]
     grid_rows = left_stat.shape[2]

time: 624 us -> 641 us (1.027)
  waiting for transfers between devices: 443 us -> 552 us
  blocking collectives: 102 us -> 0 us
    all_gather x0 -> x1, waiting for transfers between devices: none -> 107 us  [shards(): summed = jnp.sum(lax.all_gather(partial_grad, 'dp'), axis=0)]
    psum x1 -> x0, blocking collectives: 102 us -> none  [shards(): summed = lax.psum(partial_grad, 'dp')]
  transfers between devices with their start and end apart: 5 -> 6, of which waited for: 5 -> 6; matrix products, arithmetic and copies ran while one was open for 6% -> 6% of each run, Pallas kernels for 0% -> 0%
where the time goes in v1:
time: 641 us
  waiting for transfers between devices  552 us (86%)
  matrix products  53.9 us (8%)
  between operations  14.2 us (2%)
  other arithmetic  13.3 us (2%)
  local copies, waits for them, and re-layouts  7.18 us (1%)
    psum x1, waiting for transfers between devices, spread(): return lax.psum(jnp.where(mine, shard, jnp.zeros_like(shard)), axis)  155 us
    reduce_scatter x1, waiting for transfers between devices, shards(): lax.psum_scatter(jnp.einsum('pab,pbk->apk', left_root, grad_rows, preferr...  145 us
    all_gather x1, waiting for transfers between devices, shards(): summed = jnp.sum(lax.all_gather(partial_grad, 'dp'), axis=0)  107 us
    all_gather x1, waiting for transfers between devices, shards(): lax.all_gather(right_root, 'grid', axis=1, tiled=True).astype(jnp.float32)  80.4 us
    all_gather x1, waiting for transfers between devices, shards(): lax.all_gather(summed.astype(jnp.bfloat16), 'tensor', axis=2, tiled=True)  59.5 us
    dot_general x1, matrix products, shards(): jnp.einsum('pak,pbk->pab', own_rows, grad_rows, preferred_element_type=jn...  19.3 us
    dot_general x1, matrix products, shards(): jnp.einsum('pab,pbk->apk', left_root, grad_rows, preferred_element_type=j...  15.8 us
  transfers between devices with their start and end apart: 6, of which 6 were waited for; matrix products, arithmetic and copies ran while one was open for 6% of the time, Pallas kernels for 0%

profile of v1, /device:TPU:0, one launch (start us, length us, event | category | flops | bytes accessed | tf_op | source)
XLA Modules:
  0.0 640.9 jit_solution(6445191900169032796)
XLA Ops:
  7.2 0.0 copy-start
  7.2 0.0 all-gather.9.cloned.1.call-start
  7.2 1.8 copy-done
  9.1 5.0 convolution_bitcast_fusion
  14.0 5.3 copy.13
  19.4 0.0 all-gather.9.cloned.1.call-update
  19.4 0.0 all-gather.5.cloned.1.call-start
  19.4 106.8 %all-gather.9.cloned.1.call-done = f32[4,2048,256]{2,1,0:T(8,128)} async-done(((f32[2,2048,256]{2,1,0:T(8,128)}), f32[4,2048,256]{2,1,0:T(8,128)}) %all-gather.9.cloned.1.call-update) | async-done | bytes 8388624 | tf_op jit(solution)/shard_map/all_gather | solution.py:17
  126.3 6.0 reduce_sum.9
  132.2 0.0 all-gather.5.cloned.1.call-update
  132.3 0.0 all-reduce.2.cloned.1.call-start
  132.4 59.5 %all-gather.5.cloned.1.call-done = bf16[2,2048,1024]{2,1,0:T(8,128)(2,1)} async-done(((bf16[2,2048,256]{2,1,0:T(8,128)(2,1)}), bf16[2,2048,1024]{2,1,0:T(8,128)(2,1)}) %all-gather.5.cloned.1.call-update) | async-done | bytes 8388624 | tf_op jit(solution)/shard_map/all_gather | solution.py:18
  191.8 5.5 dynamic-slice_select_fusion
  197.3 0.0 all-reduce.2.cloned.1.call-update
  197.3 0.0 reduce-scatter.3.cloned.1.call-start
  197.4 155.1 %all-reduce.2.cloned.1.call-done = bf16[2,1024,1024]{2,1,0:T(8,128)(2,1)} async-done(((bf16[2,1024,1024]{2,1,0:T(8,128)(2,1)}), bf16[2,1024,1024]{2,1,0:T(8,128)(2,1)}) %all-reduce.2.cloned.1.call-update) | async-done | bytes 4194320 | tf_op jit(solution)/shard_map/psum | solution.py:12
  352.5 5.5 fusion.1
  358.0 0.0 reduce-scatter.3.cloned.1.call-update
  358.0 0.0 all-gather.7.cloned.1.call-start
  358.1 0.5 all-gather.7.cloned.1.call-update
  358.6 0.2 reduce-scatter.5.cloned.1.call-start
  358.8 15.8 %convolution_bitcast_fusion.1 = f32[1024,2,1024]{2,0,1:T(8,128)} fusion(bf16[2,1024,2048]{2,1,0:T(8,128)(2,1)} %param.11, bf16[2,2048,1024]{2,1,0:T(8,128)(2,1)} %all-gather.5.cloned.1.call-done), kind=kOutput, calls=%fused_computation.3 | convolution fusion | flops 8589934592 | bytes 25165824 | tf_op jit(solution)/shard_map/pab,pbk->apk/dot_general | solution.py:39
  374.6 0.0 reduce-scatter.5.cloned.1.call-update
  374.7 0.0 copy-start.2
  374.7 19.3 %multiply_add_fusion = f32[2,1024,2048]{2,1,0:T(8,128)} fusion(f32[2,1024,2048]{2,1,0:T(8,128)} %param.9, bf16[2,1024,1024]{2,1,0:T(8,128)(2,1)} %all-reduce.2.cloned.1.call-done, bf16[2,2048,1024]{2,1,0:T(8,128)(2,1)} %all-gather.5.cloned.1.call-done), kind=kOutput, calls=%fused_computation | convolution fusion | flops 8602517504 | bytes 46137344 | tf_op jit(solution)/shard_map/pak,pbk->pab/dot_general | solution.py:27
  394.0 4.2 reduce-scatter.3.cloned.1.call-done
  398.3 0.0 copy-done.2
  398.3 1.8 multiply_add_fusion.2
  400.1 80.4 %all-gather.7.cloned.1.call-done = bf16[2,1024,1024]{2,1,0:T(8,128)(2,1)} async-done(((bf16[2,256,1024]{2,1,0:T(8,128)(2,1)}), bf16[2,1024,1024]{2,1,0:T(8,128)(2,1)}) %all-gather.7.cloned.1.call-update) | async-done | bytes 4194320 | tf_op jit(solution)/shard_map/all_gather | solution.py:44
  480.5 145.3 %reduce-scatter.5.cloned.1.call-done = f32[256,2,1024]{2,0,1:T(8,128)} async-done(((f32[1024,2,1024]{2,0,1:T(8,128)}), f32[256,2,1024]{2,0,1:T(8,128)}) %reduce-scatter.5.cloned.1.call-update) | async-done | bytes 2097168 | tf_op jit(solution)/shard_map/reduce_scatter | solution.py:38
  625.8 8.3 %multiply_add_fusion.1 = f32[2,256,1024]{2,1,0:T(8,128)} fusion(f32[2,256,1024]{2,1,0:T(8,128)} %param.13, f32[256,2,1024]{2,0,1:T(8,128)} %reduce-scatter.5.cloned.1.call-done, bf16[2,1024,1024]{2,1,0:T(8,128)(2,1)} %all-gather.7.cloned.1.call-done), kind=kOutput, calls=%fused_computation.5 | convolution fusion | flops 6443499520 | bytes 10485760 | tf_op jit(solution)/shard_map/mpk,pkc->mpc/dot_general | solution.py:45
  634.1 0.0 copy-done.1
  (1 shorter events, 0.0 us)
Async XLA Ops:
  7.2 1.9 copy-start
  7.2 119.1 %all-gather.9.cloned.1.call-start = ((), (), s32[]{:S(2)}) async-start(), calls=%async_computation.7 | async-start | bytes 12582912 | tf_op jit(solution)/shard_map/all_gather | solution.py:17
  19.4 172.4 %all-gather.5.cloned.1.call-start = ((), (), s32[]{:S(2)}) async-start(), calls=%async_computation.2 | async-start | bytes 10485760 | tf_op jit(solution)/shard_map/all_gather | solution.py:18
  132.3 220.2 %all-reduce.2.cloned.1.call-start = ((), (), s32[]{:S(2)}) async-start(), calls=%async_computation.3 | async-start | bytes 8388608 | tf_op jit(solution)/shard_map/psum | solution.py:12
  197.3 200.9 %reduce-scatter.3.cloned.1.call-start = ((), (), s32[]{:S(2)}) async-start(), calls=%async_computation.4 | async-start | bytes 2359296 | tf_op jit(solution)/shard_map/reduce_scatter | solution.py:36
  358.0 122.5 %all-gather.7.cloned.1.call-start = ((), (), s32[]{:S(2)}) async-start(), calls=%async_computation.6 | async-start | bytes 5242880 | tf_op jit(solution)/shard_map/all_gather | solution.py:44
  358.6 267.2 %reduce-scatter.5.cloned.1.call-start = ((), (), s32[]{:S(2)}) async-start(), calls=%async_computation.5 | async-start | bytes 10485760 | tf_op jit(solution)/shard_map/reduce_scatter | solution.py:38
  374.7 23.6 %copy-start.2 = (f32[2,128,256]{2,1,0:T(8,128)S(1)}, f32[2,128,256]{2,1,0:T(8,128)}, u32[]{:S(2)}) copy-start(f32[2,128,256]{2,1,0:T(8,128)} %param.10) | copy-start | bytes 786436
  398.3 235.8 %copy-start.1 = (bf16[768,2048]{1,0:T(8,128)(2,1)S(1)}, bf16[768,2048]{1,0:T(8,128)(2,1)}, u32[]{:S(2)}) copy-start(bf16[768,2048]{1,0:T(8,128)(2,1)} %param.7) | copy-start | bytes 9437188
Sparse Core Ops, SparseCore 0:
  19.5 106.6 all-gather.8
  132.4 59.3 all-gather.4
  197.4 154.9 all-reduce.1
  358.1 40.0 reduce-scatter.2
  399.7 80.7 all-gather.6
  482.7 143.0 reduce-scatter.4
